TPU v7x, 32 devices: a whole 2x2x4 slice. The times are simulated.
32 devices in a mesh: groups: 2 (over y), shell: 8 (over z, x), batch: 2 (over core).
Axes of the slice: x: 2, y: 2, z: 4, core: 2. Of those that a mesh axis runs over, the one named last changes fastest.
Arguments:
- particles: bfloat16 [320, 1024], P(('groups', 'batch'), 'shell'), parts along dimension 0, may hold values from -5 to 5
- classes: bfloat16 [512, 1024], P('groups', 'shell'), parts along dimension 0, may hold values from -2.5 to 2.5
- ctf: float32 [16, 512], P('groups', 'shell'), parts along dimension 0, may hold values from 0.1 to 1
- sigma2: float32 [128], P('groups'), parts along dimension 0, may hold values from 0.5 to 8
- shell_of: int32 [512], P('shell'), may hold values from 0 to 63, as said below
- rot_table: int32 [48, 512], P(None, 'shell'), may hold values from 0 to 511, as said below
- ctf_group: int32 [320], P(('groups', 'batch')), parts along dimension 0, may hold values from 0 to 7
Outputs:
- class_sums: float32 [512, 1024], P('groups', 'shell'), parts along dimension 0
- class_weights: float32 [512, 512], P('groups', 'shell'), parts along dimension 0
- log_evidence: float32 [320], P(('groups', 'batch')), parts along dimension 0
There are 2 independent parts, one for each index of `groups`. A program takes and returns all parts, laid end to end along the dimension named above; an argument that names none is the same for every part. Nothing has to cross between parts.
Inputs may be any that keep to these rules, and one draw needn't show every extreme that they name: shell_of never falls along the coefficients; its first entry is 0 and its last 63. `rot_table`: for each rotation, each aligned block of 64 coefficients is mapped onto itself one to one; rotation 0 maps every coefficient to itself.
All inputs are finite; a program needn't handle non-finite values.
Results may differ from a plain program's by a relative error of at most 0.0041.
Values may be sent and summed in bfloat16 or wider, within the bound.
A program may use at most 64 MiB of HBM per device.

v0:
```python
import jax
import jax.numpy as jnp
from jax import lax
from jax.sharding import PartitionSpec as P


def body(particles, classes, ctf, sigma2, shell_of, rot_table, ctf_group):
    highest = lax.Precision.HIGHEST
    coef_width = shell_of.shape[0]
    class_count = classes.shape[0]
    rotations = rot_table.shape[0]
    levels = sigma2.shape[0]
    group_count = ctf.shape[0]
    offset = lax.axis_index("shell") * coef_width
    local_table = rot_table - offset
    pick_shell = (shell_of[:, None] == jnp.arange(levels, dtype=jnp.int32)[None, :]).astype(
        jnp.float32
    )
    weight = 1.0 / jnp.dot(
        pick_shell, sigma2, precision=highest, preferred_element_type=jnp.float32
    )
    pick_group = (ctf_group[:, None] == jnp.arange(group_count, dtype=jnp.int32)[None, :]).astype(
        jnp.float32
    )
    ctf_part = jnp.dot(pick_group, ctf, precision=highest, preferred_element_type=jnp.float32)
    values = particles.astype(jnp.float32)
    real_part = values[:, :coef_width]
    imag_part = values[:, coef_width:]
    weighted_ctf = weight[None, :] * ctf_part
    weighted = jnp.concatenate([weighted_ctf * real_part, weighted_ctf * imag_part], axis=1).astype(
        jnp.bfloat16
    )
    ctf_power = weight[None, :] * ctf * ctf
    sources = jnp.concatenate(
        [ctf_part * real_part, ctf_part * imag_part, ctf_part * ctf_part], axis=1
    ).astype(jnp.bfloat16)
    class_view = classes.reshape(class_count, 2, coef_width)
    rotated = jnp.take(class_view, local_table, axis=2)
    rotated = jnp.transpose(rotated, (0, 2, 1, 3)).reshape(class_count * rotations, 2 * coef_width)
    cross_terms = lax.dot_general(
        weighted, rotated, (((1,), (1,)), ((), ())), preferred_element_type=jnp.float32
    )
    rot_float = rotated.astype(jnp.float32)
    class_power = rot_float[:, :coef_width] ** 2 + rot_float[:, coef_width:] ** 2
    penalty = lax.dot_general(
        ctf_power,
        class_power,
        (((1,), (1,)), ((), ())),
        precision=highest,
        preferred_element_type=jnp.float32,
    )
    total = lax.psum(
        cross_terms
        - 0.5 * jnp.dot(pick_group, penalty, precision=highest, preferred_element_type=jnp.float32),
        "shell",
    )
    peak = jnp.max(total, axis=1)
    log_evidence = peak + jnp.log(jnp.sum(jnp.exp(total - peak[:, None]), axis=1))
    posterior = jnp.exp(total - log_evidence[:, None]).astype(jnp.bfloat16)
    frames = lax.dot_general(
        posterior, sources, (((0,), (0,)), ((), ())), preferred_element_type=jnp.float32
    )
    frames = frames.reshape(class_count, rotations, 3, coef_width)
    placing = (
        local_table[:, :, None] == jnp.arange(coef_width, dtype=jnp.int32)[None, None, :]
    ).astype(jnp.float32)
    unrotated = jnp.einsum(
        "krqc,rcd->kqd", frames, placing, precision=highest, preferred_element_type=jnp.float32
    )
    sums_part = unrotated[:, 0:2].reshape(class_count, 2 * coef_width)
    weights_part = unrotated[:, 2]
    class_sums, class_weights = lax.psum((sums_part, weights_part), "batch")
    return (class_sums, class_weights, log_evidence)


def solution(mesh):
    in_specs = (
        P(("groups", "batch"), "shell"),
        P("groups", "shell"),
        P("groups", "shell"),
        P("groups"),
        P("shell"),
        P(None, "shell"),
        P(("groups", "batch")),
    )
    out_specs = (P("groups", "shell"), P("groups", "shell"), P(("groups", "batch")))
    return jax.shard_map(body, mesh=mesh, in_specs=in_specs, out_specs=out_specs, check_vma=False)
```

profile of v0, /device:TPU:0, one launch (start us, length us, event | category | flops | bytes accessed | tf_op | source)
XLA Modules:
  0.0 281.5 jit_solution(13921262541019871382)
XLA Ops:
  7.2 0.8 copy.13
  8.1 0.8 compare_and_fusion
  8.9 0.9 copy.14
  10.0 11.7 %gather_fusion = bf16[3072,256,2]{1,2,0:T(2,128)(2,1)S(1)} fusion(bf16[256,2,64]{0,1,2:T(2,128)(2,1)S(1)} %copy.15, s32[3072]{0:T(1024)S(1)} %broadcast_clamp_fusion), kind=kCustom, calls=%fused_computation | custom fusion | bytes 6303744 | tf_op jit(solution)/shard_map/jit(_take)/gather | solution.py:38
  21.6 0.5 copy.16
  22.1 0.6 select_bitcast_fusion
  22.7 10.8 %copy.17 = bf16[256,48,2,64]{3,2,1,0:T(2,128)(2,1)} copy(bf16[256,48,2,64]{0,3,1,2:T(8,128)(2,1)S(1)} %select_bitcast_fusion) | data formatting | bytes 6291456 | tf_op jit(solution)/shard_map/jit(_take)/select_n | solution.py:38
  33.5 9.8 %reshape.35 = bf16[12288,128]{1,0:T(8,128)(2,1)S(1)} reshape(bf16[256,48,2,64]{3,2,1,0:T(2,128)(2,1)} %copy.17) | data formatting | bytes 6291456 | tf_op jit(solution)/shard_map/reshape | solution.py:39
  43.3 0.5 convert_element_type.7
  44.1 5.9 %fusion.2 = f32[8,12288]{1,0:T(8,128)S(1)} fusion(f32[12288,128]{1,0:T(8,128)S(1)} %convert_element_type.7, f32[8,64]{1,0:T(8,128)S(1)} %copy-done.5, f32[64]{0:T(128)S(1)} %fusion.7), kind=kOutput, calls=%fused_computation.5 | convolution fusion | flops 77857792 | bytes 12980736 | tf_op jit(solution)/shard_map/dot_general | solution.py:45
  50.3 1.2 fusion.14
  51.5 4.0 %fusion = f32[80,12288]{1,0:T(8,128)} fusion(f32[80,12288]{1,0:T(8,128)S(1)} %fusion.14, f32[8,12288]{1,0:T(8,128)S(1)} %fusion.2, s32[80]{0:T(128)S(1)} %copy-done.3), kind=kOutput, calls=%fused_computation.2 | convolution fusion | flops 96338560 | bytes 8257856 | tf_op jit(solution)/shard_map/dot_general | solution.py:54
  56.0 0.9 copy.21
  56.8 151.0 %all-reduce.4.cloned.1.call-done = f32[80,12288]{1,0:T(8,128)} async-done(((f32[80,12288]{1,0:T(8,128)}), f32[80,12288]{1,0:T(8,128)}) %all-reduce.4.cloned.1.call-update) | async-done | bytes 3932176 | tf_op jit(solution)/shard_map/psum | solution.py:52
  207.9 2.4 reduce_max.9
  210.3 2.9 %exponential_reduce_fusion = f32[80]{0:T(128)S(1)} fusion(f32[80,12288]{1,0:T(8,128)} %all-reduce.4.cloned.1.call-done, f32[80]{0:T(128)S(1)} %reduce_max.9), kind=kLoop, calls=%fused_computation.8 | loop fusion | flops 1966000 | bytes 3932800 | tf_op jit(solution)/shard_map/reduce_sum | solution.py:58
  213.6 5.0 %fusion.4 = f32[12288,192]{0,1:T(8,128)} fusion(f32[80,12288]{1,0:T(8,128)S(1)} %copy-done.2, f32[80]{0:T(128)S(1)} %log_add_fusion, bf16[80,64]{0,1:T(8,128)(2,1)S(1)} %get-tuple-element.13, bf16[80,64]{0,1:T(8,128)(2,1)S(1)} %get-tuple-element.10, bf16[80,64]{0,1:T(8,128)(2,1)S(1)} %get-tuple-element.9), kind=kOutput, calls=%fused_computation.10 | convolution fusion | flops 379545600 | bytes 13400384 | tf_op jit(solution)/shard_map/dot_general | solution.py:60
  218.6 17.9 %reshape.36 = f32[256,48,3,64]{1,0,3,2:T(8,128)} reshape(f32[12288,192]{0,1:T(8,128)} %fusion.4) | data formatting | bytes 18874368 | tf_op jit(solution)/shard_map/reshape | solution.py:63
  236.4 16.4 %convolution_bitcast_fusion = f32[256,3,64]{0,2,1:T(8,128)S(1)} fusion(f32[256,48,3,64]{1,0,3,2:T(8,128)} %reshape.36, pred[48,64,64,1]{2,0,1,3:T(8,128)(4,1)S(1)} %copy.21), kind=kOutput, calls=%fused_computation.14 | convolution fusion | flops 1811939328 | bytes 9830400 | tf_op jit(solution)/shard_map/krqc,rcd->kqd/dot_general | solution.py:67
  252.9 0.6 slice_bitcast_fusion
  253.5 0.8 copy.19
  254.3 17.3 %all-reduce.6.cloned.1.call-done = (f32[256,128]{1,0:T(8,128)}, f32[256,64]{0,1:T(8,128)}) async-done(((f32[256,128]{1,0:T(8,128)}, f32[256,64]{0,1:T(8,128)}), (f32[256,128]{1,0:T(8,128)}, f32[256,64]{0,1:T(8,128)})) %all-reduce.6.cloned.1.call-update) | async-done | bytes 196624 | tf_op jit(solution)/shard_map/psum | solution.py:72
  271.6 1.6 copy.26
  273.2 1.5 copy.27
  (28 shorter events, 1.7 us)
Async XLA Ops:
  7.2 36.6 %copy-start = (f32[64]{0:T(128)S(1)}, f32[64]{0:T(128)}, u32[]{:S(2)}) copy-start(f32[64]{0:T(128)} %param.10) | copy-start | bytes 772
  7.2 200.7 %all-reduce.4.cloned.1.call-start = ((), (), s32[]{:S(2)}) async-start(), calls=%async_computation | async-start | bytes 7864320 | tf_op jit(solution)/shard_map/psum | solution.py:52
  43.3 0.7 copy-start.6
  43.3 0.8 copy-start.5
  43.9 6.1 %copy-start.3 = (s32[80]{0:T(128)S(1)}, s32[80]{0:T(128)}, u32[]{:S(2)}) copy-start(s32[80]{0:T(128)} %param.13) | copy-start | bytes 964
  55.5 216.1 %all-reduce.6.cloned.1.call-start = ((), (), s32[]{:S(2)}) async-start(), calls=%async_computation.1 | async-start | bytes 393216 | tf_op jit(solution)/shard_map/psum | solution.py:72
  210.2 3.3 %copy-start.2 = (f32[80,12288]{1,0:T(8,128)S(1)}, f32[80,12288]{1,0:T(8,128)}, u32[]{:S(2)}) copy-start(f32[80,12288]{1,0:T(8,128)} %all-reduce.4.cloned.1.call-done) | copy-start | bytes 11796484
  213.2 5.4 %copy-start.4 = (f32[80]{0:T(128)}, f32[80]{0:T(128)S(1)}, u32[]{:S(2)}) copy-start(f32[80]{0:T(128)S(1)} %log_add_fusion) | copy-start | bytes 964
  236.4 38.2 %copy-start.1 = (f32[64]{0:T(128)S(1)}, f32[64]{0:T(128)}, u32[]{:S(2)}) copy-start(f32[64]{0:T(128)} %param.10) | copy-start | bytes 772
Sparse Core Ops, SparseCore 0:
  55.6 152.1 all-reduce.3
  254.4 17.1 all-reduce.5
where the time goes:
time: 282 us
  waiting for transfers between devices  168 us (60%)
  local copies, waits for them, and re-layouts  58.3 us (21%)
  matrix products  33 us (12%)
  between operations  14.2 us (5%)
  other arithmetic  7.38 us (3%)
    psum x1, waiting for transfers between devices, body(): lax.psum(cross_terms - 0.5 * jnp.dot(pick_group, penalty, precision=highe...  151 us
    reshape x1, local copies, waits for them, and re-layouts, body(): frames = frames.reshape(class_count, rotations, 3, coef_width)  17.9 us
    psum x1, waiting for transfers between devices, body(): class_sums, class_weights = lax.psum((sums_part, weights_part), 'batch')  17.3 us
    dot_general x1, matrix products, body(): jnp.einsum('krqc,rcd->kqd', frames, placing, precision=highest, preferred...  16.4 us
    gather x2, local copies, waits for them, and re-layouts, body(): rotated = jnp.take(class_view, local_table, axis=2)  12.1 us
    select_n x1, local copies, waits for them, and re-layouts, body(): rotated = jnp.take(class_view, local_table, axis=2)  10.8 us
    reshape x1, local copies, waits for them, and re-layouts, body(): jnp.transpose(rotated, (0, 2, 1, 3))  9.77 us
    dot_general x1, matrix products, body(): lax.dot_general(ctf_power, class_power, (((1,), (1,)), ((), ())), precisi...  5.89 us
  transfers between devices with their start and end apart: 2, of which 2 were waited for; matrix products, arithmetic and copies ran while one was open for 0% of the time, Pallas kernels for 0%

commit v1 on v0

v1 whole, which is shorter than its diff:
```python
import functools

import jax
import jax.numpy as jnp
from jax import lax
from jax.experimental import pallas as pl
from jax.experimental.pallas import tpu as pltpu
from jax.sharding import PartitionSpec as P

MESH = pl.DeviceIdType.MESH
BF16 = jnp.bfloat16
F32 = jnp.float32


def plain_body(particles, classes, ctf, sigma2, shell_of, rot_table, ctf_group):
    highest = lax.Precision.HIGHEST
    coef_width = shell_of.shape[0]
    class_count = classes.shape[0]
    rotations = rot_table.shape[0]
    levels = sigma2.shape[0]
    group_count = ctf.shape[0]
    offset = lax.axis_index("shell") * coef_width
    local_table = rot_table - offset
    pick_shell = (shell_of[:, None] == jnp.arange(levels, dtype=jnp.int32)[None, :]).astype(F32)
    weight = 1.0 / jnp.dot(pick_shell, sigma2, precision=highest, preferred_element_type=F32)
    pick_group = (ctf_group[:, None] == jnp.arange(group_count, dtype=jnp.int32)[None, :]).astype(F32)
    ctf_part = jnp.dot(pick_group, ctf, precision=highest, preferred_element_type=F32)
    values = particles.astype(F32)
    real_part = values[:, :coef_width]
    imag_part = values[:, coef_width:]
    weighted_ctf = weight[None, :] * ctf_part
    weighted = jnp.concatenate([weighted_ctf * real_part, weighted_ctf * imag_part], axis=1).astype(BF16)
    ctf_power = weight[None, :] * ctf * ctf
    sources = jnp.concatenate(
        [ctf_part * real_part, ctf_part * imag_part, ctf_part * ctf_part], axis=1
    ).astype(BF16)
    class_view = classes.reshape(class_count, 2, coef_width)
    rotated = jnp.take(class_view, local_table, axis=2)
    rotated = jnp.transpose(rotated, (0, 2, 1, 3)).reshape(class_count * rotations, 2 * coef_width)
    cross_terms = lax.dot_general(
        weighted, rotated, (((1,), (1,)), ((), ())), preferred_element_type=F32
    )
    rot_float = rotated.astype(F32)
    class_power = rot_float[:, :coef_width] ** 2 + rot_float[:, coef_width:] ** 2
    penalty = lax.dot_general(
        ctf_power, class_power, (((1,), (1,)), ((), ())), precision=highest, preferred_element_type=F32
    )
    total = lax.psum(
        cross_terms - 0.5 * jnp.dot(pick_group, penalty, precision=highest, preferred_element_type=F32),
        "shell",
    )
    peak = jnp.max(total, axis=1)
    log_evidence = peak + jnp.log(jnp.sum(jnp.exp(total - peak[:, None]), axis=1))
    posterior = jnp.exp(total - log_evidence[:, None]).astype(BF16)
    frames = lax.dot_general(
        posterior, sources, (((0,), (0,)), ((), ())), preferred_element_type=F32
    )
    frames = frames.reshape(class_count, rotations, 3, coef_width)
    placing = (
        local_table[:, :, None] == jnp.arange(coef_width, dtype=jnp.int32)[None, None, :]
    ).astype(F32)
    unrotated = jnp.einsum(
        "krqc,rcd->kqd", frames, placing, precision=highest, preferred_element_type=F32
    )
    sums_part = unrotated[:, 0:2].reshape(class_count, 2 * coef_width)
    weights_part = unrotated[:, 2]
    class_sums, class_weights = lax.psum((sums_part, weights_part), "batch")
    return (class_sums, class_weights, log_evidence)


def split3(x):
    one = x.astype(BF16).astype(F32)
    two = (x - one).astype(BF16).astype(F32)
    return one, two, x - one - two


def gather_lanes(x, index):
    return jnp.take_along_axis(x, index, axis=1, mode="promise_in_bounds")


def kernel(
    n, m, kc, rot, part_ref, tab_ref, cls_ref, cw_ref, pick_ref,
    sums_ref, wts_ref, logev_ref,
    g_part, g_tab, g_cls, g_cw, g_pick, fwd, inv, cls32, w_s, s_s, p_s, r_s, hi_s, lo_s, sc_s, post_s, frame,
    st_mine, st_all, o_mine, o_all,
    in_send, in_recv, relay_send, relay_recv, pick_sem, st_send, st_recv, o_send, o_recv,
):
    s = lax.axis_index("shell")
    b = lax.axis_index("batch")
    rows = part_ref.shape[0]
    total_rows = m * rows
    half = 64
    me = s * m + b
    nd = n * m
    lane = lambda shape: lax.broadcasted_iota(jnp.int32, shape, len(shape) - 1)

    def peer(o):
        other = lax.rem(me + o, nd)
        return other, {"shell": other // m, "batch": lax.rem(other, m)}

    barrier = pltpu.get_barrier_semaphore()
    for o in range(1, nd):
        pl.semaphore_signal(barrier, inc=1, device_id=peer(o)[1], device_id_type=MESH)
    pl.semaphore_wait(barrier, nd - 1)

    copies = []
    for o in range(1, n):
        t = lax.rem(s + o, n)
        dest = {"shell": t, "batch": b}
        first = pl.multiple_of((t * m + b) * kc, kc)
        pairs = (
            (cls_ref.at[pl.ds(first, kc)], g_cls.at[s]),
            (cw_ref, g_cw.at[s]),
            (tab_ref, g_tab.at[s]),
            (part_ref, g_part.at[b, s]),
        )
        for j, (src, dst) in enumerate(pairs):
            copy = pltpu.make_async_remote_copy(
                src_ref=src, dst_ref=dst, send_sem=in_send.at[j, t], recv_sem=in_recv.at[j, s],
                device_id=dest, device_id_type=MESH,
            )
            copy.start()
            copies.append(copy)
    partner = {"shell": s, "batch": 1 - b}
    pick_copy = pltpu.make_async_remote_copy(
        src_ref=pick_ref, dst_ref=g_pick.at[b], send_sem=pick_sem.at[0], recv_sem=pick_sem.at[1],
        device_id=partner, device_id_type=MESH,
    )
    pick_copy.start()
    relays = []

    def relay(src, t):
        copy = pltpu.make_async_remote_copy(
            src_ref=src, dst_ref=g_part.at[b, t], send_sem=relay_send.at[t], recv_sem=relay_recv.at[t],
            device_id=partner, device_id_type=MESH,
        )
        copy.start()
        relays.append(copy)

    relay(part_ref, s)
    g_part[b, s] = part_ref[...]
    g_pick[b] = pick_ref[...]
    g_tab[s] = tab_ref[...]
    g_cw[s] = cw_ref[...]
    g_cls[s] = cls_ref[pl.ds(pl.multiple_of(me * kc, kc), kc), :]

    def arrive(j, t):
        refs = (g_cls.at[t], g_cw.at[t], g_tab.at[t], g_part.at[b, t])
        pltpu.make_async_remote_copy(
            src_ref=refs[j], dst_ref=refs[j], send_sem=in_send.at[j, t], recv_sem=in_recv.at[j, t],
            device_id=partner, device_id_type=MESH,
        ).wait_recv()

    for o in range(1, n):
        t = lax.rem(s + n - o, n)
        arrive(0, t)
        arrive(1, t)
        arrive(2, t)
    for o in range(1, n):
        t = lax.rem(s + n - o, n)
        arrive(3, t)
        relay(g_part.at[b, t], t)

    left = lane((rot, 128)) < half
    for t in range(n):
        tab = g_tab[t].astype(F32)
        swap = pltpu.roll(tab, half, 1)
        fwd[t] = jnp.where(left, tab, swap + half).astype(jnp.int32)
        inv[t] = jnp.where(left, swap, tab + half).astype(jnp.int32)
        cls32[t] = g_cls[t].astype(F32)

    def rotate(r, carry):
        at = pl.ds(pl.multiple_of(r * kc, kc), kc)
        for t in range(n):
            index = jnp.broadcast_to(fwd[t, pl.ds(r, 1), :], (kc, 128))
            turned = gather_lanes(cls32[t], index)
            square = turned * turned
            high = square.astype(BF16)
            cols = slice(t * 128, t * 128 + 128)
            r_s[at, cols] = turned.astype(BF16)
            hi_s[at, cols] = high
            lo_s[at, cols] = (square - high.astype(F32)).astype(BF16)
        return carry

    lax.fori_loop(0, rot, rotate, 0)

    pick_copy.wait()
    for o in range(n):
        t = lax.rem(s + o, n)
        pltpu.make_async_remote_copy(
            src_ref=g_part.at[1 - b, t], dst_ref=g_part.at[1 - b, t],
            send_sem=relay_send.at[t], recv_sem=relay_recv.at[t],
            device_id=partner, device_id_type=MESH,
        ).wait_recv()

    pick = g_pick[...].reshape(total_rows, 128)[:, :32]
    left8 = lane((8, 128)) < half
    left_p = lane((total_rows, 128)) < half
    before = None
    for t in range(n):
        packed = g_cw[t]
        swap = pltpu.roll(packed, half, 1)
        ctf = jnp.where(left8, packed, swap)
        weight = jnp.where(left8, swap, packed)
        zero = jnp.zeros_like(ctf)
        pieces = jnp.concatenate(split3(ctf) + (zero,), axis=0).astype(BF16)
        ctf_part = jnp.dot(pick, pieces, preferred_element_type=F32)
        values = g_part[:, t].reshape(total_rows, 128).astype(F32)
        cols = slice(t * 128, t * 128 + 128)
        w_s[:, cols] = (weight[0:1] * ctf_part * values).astype(BF16)
        s_s[:, cols] = (ctf_part * values).astype(BF16)
        p_s[:, cols] = jnp.concatenate(split3(weight * ctf * ctf) + (zero,), axis=0).astype(BF16)
        if t % 2 == 1:
            mixed = jnp.where(left_p, before, ctf_part)
            cols = slice(n * 128 + t // 2 * 128, n * 128 + t // 2 * 128 + 128)
            s_s[:, cols] = (mixed * mixed).astype(BF16)
        before = ctf_part

    nt = (((1,), (1,)), ((), ()))
    chunk = 128
    big = kc * rot

    def score(i, peak):
        at = pl.ds(pl.multiple_of(i * chunk, chunk), chunk)
        cross = lax.dot_general(r_s[at, :], w_s[...], nt, preferred_element_type=F32)
        pen = lax.dot_general(hi_s[at, :], p_s[...], nt, preferred_element_type=F32)
        pen = pen + lax.dot_general(lo_s[at, :], p_s[...], nt, preferred_element_type=F32)
        spread = 0.0
        for piece in split3(pen):
            spread = spread + lax.dot_general(piece.astype(BF16), pick, nt, preferred_element_type=F32)
        total = cross - 0.5 * spread
        sc_s[at, :] = total
        return jnp.maximum(peak, jnp.max(total, axis=0, keepdims=True))

    peak = lax.fori_loop(0, big // chunk, score, jnp.full((1, total_rows), -jnp.inf, F32))
    summed = jnp.sum(jnp.exp(sc_s[...] - peak), axis=0, keepdims=True)
    st_mine[0:1, :] = peak
    st_mine[1:2, :] = summed
    st_mine[2:8, :] = jnp.zeros((6, total_rows), F32)

    sends = []
    for o in range(1, nd):
        other, dest = peer(o)
        copy = pltpu.make_async_remote_copy(
            src_ref=st_mine, dst_ref=st_all.at[me], send_sem=st_send.at[other], recv_sem=st_recv.at[me],
            device_id=dest, device_id_type=MESH,
        )
        copy.start()
        sends.append(copy)
    st_all[me] = st_mine[...]
    for o in range(1, nd):
        other = lax.rem(me + nd - o, nd)
        pltpu.make_async_remote_copy(
            src_ref=st_mine, dst_ref=st_all.at[other], send_sem=st_send.at[other], recv_sem=st_recv.at[other],
            device_id=partner, device_id_type=MESH,
        ).wait_recv()
    peaks = st_all[:, 0, :]
    top = jnp.max(peaks, axis=0, keepdims=True)
    whole = jnp.sum(st_all[:, 1, :] * jnp.exp(peaks - top), axis=0, keepdims=True)
    logev = top + jnp.log(whole)
    logev_ref[...] = logev
    post_s[...] = jnp.exp(sc_s[...] - logev).astype(BF16)

    def back(first, index_of):
        cols = slice(first, first + 256)
        frame[...] = jnp.dot(post_s[...], s_s[:, cols], preferred_element_type=F32)

        def step(r, carry):
            at = pl.ds(pl.multiple_of(r * kc, kc), kc)
            out = []
            for q in range(2):
                index = jnp.broadcast_to(index_of(q, r), (kc, 128))
                out.append(carry[q] + gather_lanes(frame[at, q * 128 : q * 128 + 128], index))
            return tuple(out)

        zero = jnp.zeros((kc, 128), F32)
        return lax.fori_loop(0, rot, step, (zero, zero))

    left1 = lane((1, 128)) < half
    for j in range(n // 2):
        done = back(j * 256, lambda q, r: inv[2 * j + q, pl.ds(r, 1), :])
        for q in range(2):
            o_mine[2 * j + q, 0:kc, :] = done[q].astype(BF16)
    left_h = lane((kc // 2, 128)) < half
    for j in range(n // 4):
        done = back(
            n * 128 + j * 256,
            lambda q, r: jnp.where(
                left1, inv[4 * j + 2 * q, pl.ds(r, 1), :], inv[4 * j + 2 * q + 1, pl.ds(r, 1), :]
            ),
        )
        for q in range(2):
            low, high = done[q][: kc // 2], done[q][kc // 2 :]
            at = slice(kc, kc + kc // 2)
            o_mine[4 * j + 2 * q, at, :] = jnp.where(left_h, low, pltpu.roll(high, half, 1)).astype(BF16)
            o_mine[4 * j + 2 * q + 1, at, :] = jnp.where(left_h, pltpu.roll(low, half, 1), high).astype(BF16)

    for o in range(1, nd):
        other, dest = peer(o)
        copy = pltpu.make_async_remote_copy(
            src_ref=o_mine.at[dest["shell"]], dst_ref=o_all.at[me], send_sem=o_send.at[other],
            recv_sem=o_recv.at[me], device_id=dest, device_id_type=MESH,
        )
        copy.start()
        sends.append(copy)
    o_all[me] = o_mine[s]
    for o in range(1, nd):
        other = lax.rem(me + nd - o, nd)
        pltpu.make_async_remote_copy(
            src_ref=o_mine.at[0], dst_ref=o_all.at[other], send_sem=o_send.at[other],
            recv_sem=o_recv.at[other], device_id=partner, device_id_type=MESH,
        ).wait_recv()
    for d in range(nd):
        sums_ref[d * kc : d * kc + kc, :] = o_all[d, 0:kc, :].astype(F32)
        packed = o_all[d, kc : kc + kc // 2, :].astype(F32)
        wts_ref[d * kc : d * kc + kc // 2, :] = packed[:, :half]
        wts_ref[d * kc + kc // 2 : d * kc + kc, :] = pltpu.roll(packed, half, 1)[:, :half]
    for copy in copies + relays + sends:
        copy.wait_send()


def fast_body(n, m, particles, classes, ctf, sigma2, shell_of, rot_table, ctf_group):
    width = shell_of.shape[0]
    rot = rot_table.shape[0]
    rows = particles.shape[0]
    k = classes.shape[0]
    groups = ctf.shape[0]
    kc = k // (n * m)
    table = rot_table - lax.axis_index("shell") * width
    spots = jnp.arange(width, dtype=jnp.int32)
    inverse = jnp.sum(
        jnp.where(table[:, :, None] == spots[None, None, :], spots[None, :, None], 0), axis=1
    )
    tabs = jnp.concatenate([table, inverse], axis=1).astype(BF16)
    levels = jnp.arange(sigma2.shape[0], dtype=jnp.int32)
    chosen = jnp.sum(jnp.where(shell_of[:, None] == levels[None, :], sigma2[None, :], 0.0), axis=1)
    weight = 1.0 / chosen
    cw = jnp.concatenate([ctf, jnp.broadcast_to(weight[None, :], ctf.shape)], axis=1)
    lanes = jnp.arange(128, dtype=jnp.int32)
    pick = ((ctf_group[:, None] == (lanes % groups)[None, :]) & (lanes < 3 * groups)[None, :]).astype(BF16)
    total_rows = m * rows
    big = kc * rot
    nd = n * m
    wide = n * 128
    vmem = pl.BlockSpec(memory_space=pltpu.VMEM)
    dma = pltpu.SemaphoreType.DMA
    sums, wts, logev = pl.pallas_call(
        functools.partial(kernel, n, m, kc, rot),
        out_shape=(
            jax.ShapeDtypeStruct((k, 128), F32),
            jax.ShapeDtypeStruct((k, width), F32),
            jax.ShapeDtypeStruct((1, total_rows), F32),
        ),
        in_specs=[vmem] * 5,
        out_specs=(vmem,) * 3,
        scratch_shapes=[
            pltpu.VMEM((m, n, rows, 128), BF16),
            pltpu.VMEM((n, rot, 128), BF16),
            pltpu.VMEM((n, kc, 128), BF16),
            pltpu.VMEM((n, groups, 128), F32),
            pltpu.VMEM((m, rows, 128), BF16),
            pltpu.VMEM((n, rot, 128), jnp.int32),
            pltpu.VMEM((n, rot, 128), jnp.int32),
            pltpu.VMEM((n, kc, 128), F32),
            pltpu.VMEM((total_rows, wide), BF16),
            pltpu.VMEM((total_rows, wide + wide // 2), BF16),
            pltpu.VMEM((4 * groups, wide), BF16),
            pltpu.VMEM((big, wide), BF16),
            pltpu.VMEM((big, wide), BF16),
            pltpu.VMEM((big, wide), BF16),
            pltpu.VMEM((big, total_rows), F32),
            pltpu.VMEM((big, total_rows), BF16),
            pltpu.VMEM((big, 256), F32),
            pltpu.VMEM((8, total_rows), F32),
            pltpu.VMEM((nd, 8, total_rows), F32),
            pltpu.VMEM((n, kc + kc // 2, 128), BF16),
            pltpu.VMEM((nd, kc + kc // 2, 128), BF16),
            dma((4, n)),
            dma((4, n)),
            dma((n,)),
            dma((n,)),
            dma((2,)),
            dma((nd,)),
            dma((nd,)),
            dma((nd,)),
            dma((nd,)),
        ],
        compiler_params=pltpu.CompilerParams(
            collective_id=0, has_side_effects=True, vmem_limit_bytes=48 * 1024 * 1024
        ),
    )(particles, tabs, classes, cw, pick)
    mine = lax.dynamic_slice(logev[0], (lax.axis_index("batch") * rows,), (rows,))
    return sums, wts, mine


def solution(mesh):
    in_specs = (
        P(("groups", "batch"), "shell"),
        P("groups", "shell"),
        P("groups", "shell"),
        P("groups"),
        P("shell"),
        P(None, "shell"),
        P(("groups", "batch")),
    )
    out_specs = (P("groups", "shell"), P("groups", "shell"), P(("groups", "batch")))
    n = mesh.shape["shell"]
    m = mesh.shape["batch"]

    def body(particles, classes, ctf, sigma2, shell_of, rot_table, ctf_group):
        args = (particles, classes, ctf, sigma2, shell_of, rot_table, ctf_group)
        per = classes.shape[0] // (n * m)
        fits = (
            m == 2
            and n % 4 == 0
            and n <= 16
            and classes.shape[0] % (n * m) == 0
            and per % 16 == 0
            and shell_of.shape[0] == 64
            and ctf.shape[0] == 8
            and particles.shape[0] % 16 == 0
            and rot_table.shape[0] % 8 == 0
            and per * rot_table.shape[0] % 128 == 0
        )
        if fits:
            return fast_body(n, m, *args)
        return plain_body(*args)

    return jax.shard_map(body, mesh=mesh, in_specs=in_specs, out_specs=out_specs, check_vma=False)
```

time: 282 us -> 65 us (0.23)
  waiting for transfers between devices: 168 us -> 0 us
  Pallas kernels: 0 us -> 58.3 us
  local copies, waits for them, and re-layouts: 58.3 us -> 2.04 us
  matrix products: 33 us -> 0 us
  between operations: 14.2 us -> 0.7 us
  other arithmetic: 7.38 us -> 3.72 us
    psum x2 -> x0, waiting for transfers between devices: 168 us -> none  [the longest x1 151 us: body(): lax.psum(cross_terms - 0.5 * jnp.dot(pick_group, penalty, precision=highe...]
    pallas_call x0 -> x1, Pallas kernels: none -> 58.3 us  [fast_body(): pl.pallas_call(functools.partial(kernel, n, m, kc, rot), out_shape=(jax.S...]
    dot_general x7 -> x0, matrix products: 33 us -> none  [the longest x1 16.4 us: body(): jnp.einsum('krqc,rcd->kqd', frames, placing, precision=highest, preferred...]
    reshape x4 -> x0, local copies, waits for them, and re-layouts: 28.4 us -> none  [the longest x1 17.9 us: body(): frames = frames.reshape(class_count, rotations, 3, coef_width)]
    gather x2 -> x0, local copies, waits for them, and re-layouts: 12.1 us -> none  [body(): rotated = jnp.take(class_view, local_table, axis=2)]
    select_n x1 -> x0, local copies, waits for them, and re-layouts: 10.8 us -> none  [body(): rotated = jnp.take(class_view, local_table, axis=2)]
    unnamed x18 -> x6, local copies, waits for them, and re-layouts: 5.32 us -> 1.38 us
  transfers between devices with their start and end apart: 2 -> 0, of which waited for: 2 -> 0; matrix products, arithmetic and copies ran while one was open for 0% -> 0% of each run, Pallas kernels for 0% -> 0%
where the time goes in v1:
time: 65 us; the launch traced here: 64.8 us
  Pallas kernels  58.3 us (90%)
  other arithmetic  3.72 us (6%)
  local copies, waits for them, and re-layouts  2.04 us (3%)
  between operations  0.7 us (1%)
    pallas_call x1, Pallas kernels, fast_body(): pl.pallas_call(functools.partial(kernel, n, m, kc, rot), out_shape=(jax.S...  58.3 us
    unnamed x6, local copies, waits for them, and re-layouts  1.38 us

profile of v1, /device:TPU:0, one launch (start us, length us, event | category | flops | bytes accessed | tf_op | source)
XLA Modules:
  0.0 64.8 jit_solution(10694109944497757985)
XLA Ops:
  0.6 0.0 copy-start
  0.6 0.0 copy-start.1
  0.7 0.9 %select_reduce_fusion.1 = f32[64]{0:T(128)S(1)} fusion(f32[64]{0:T(128)} %param.10, s32[64]{0:T(128)} %param.11), kind=kLoop, calls=%fused_computation.3 | loop fusion | flops 12224 | bytes 768 | tf_op jit(solution)/shard_map/reduce_sum | solution.py:336
  1.6 0.1 pad.1.clone
  1.6 0.7 %pad_maximum_fusion.1.cw_ref = f32[8,128]{1,0:T(8,128)S(1)} fusion(f32[8,64]{1,0:T(8,128)} %param.9, f32[128]{0:T(128)S(1)} %pad.1.clone), kind=kLoop, calls=%fused_computation.7 | loop fusion | flops 1024 | bytes 6656 | tf_op jit(solution)/shard_map/concatenate | solution.py:338
  2.3 0.7 %and_convert_fusion.pick_ref = bf16[80,128]{1,0:T(8,128)(2,1)S(1)} fusion(s32[128]{0:T(128)S(1)} %and_select_fusion, s32[80]{0:T(128)} %param.13, pred[128]{0:T(512)(128)(4,1)S(1)} %iota_compare_fusion.2), kind=kLoop, calls=%fused_computation.2 | loop fusion | flops 30720 | bytes 21440 | tf_op jit(solution)/shard_map/convert_element_type | solution.py:340
  3.1 0.7 %fusion = (bf16[48,64]{1,0:T(8,128)(2,1)S(1)}, s32[48,64]{1,0:T(8,128)S(1)}) fusion(s32[48,64]{1,0:T(8,128)} %param.12, s32[]{:T(128)S(6)} %mul.6), kind=kLoop, calls=%fused_computation.12 | loop fusion | flops 6144 | bytes 30724 | tf_op jit(solution)/shard_map/convert
  3.8 0.6 select_reduce_fusion
  4.4 0.1 pad_maximum_fusion.tab_ref
  4.5 0.0 copy-done
  4.5 0.0 copy-done.1
  4.5 58.3 %shard_map.94 = (f32[256,128]{1,0:T(8,128)S(1)}, f32[256,64]{1,0:T(8,128)S(1)}, f32[1,160]{1,0:T(1,128)S(1)}) custom-call(bf16[80,128]{1,0:T(8,128)(2,1)S(1)} %copy-done.1, bf16[48,128]{1,0:T(8,128)(2,1)S(1)} %pad_maximum_fusion.tab_ref, bf16[256,128]{1,0:T(8,128)(2,1)S(1)} %copy-done, f32[8,128]{1,0:T(8,128)S(1)} %pad_maximum_fusion.1.cw_ref, ...), custom_call_target="tpu_custom_call" | custom-call | tf_op jit(solution)/shard_map/pallas_call | solution.py:347
  62.8 0.6 dynamic-slice_bitcast_fusion
  63.4 0.7 %copy.11 = f32[256,64]{0,1:T(8,128)} copy(f32[256,64]{1,0:T(8,128)S(1)} %get-tuple-element.13) | data formatting | bytes 131072
  64.1 0.7 %copy.13 = f32[256,128]{1,0:T(8,128)} copy(f32[256,128]{1,0:T(8,128)S(1)} %get-tuple-element.20) | data formatting | bytes 262144
  (4 shorter events, 0.0 us)
Async XLA Ops:
  0.6 3.9 %copy-start = (bf16[256,128]{1,0:T(8,128)(2,1)S(1)}, bf16[256,128]{1,0:T(8,128)(2,1)}, u32[]{:S(2)}) copy-start(bf16[256,128]{1,0:T(8,128)(2,1)} %cls_ref.1) | copy-start | bytes 196612
  0.6 3.9 %copy-start.1 = (bf16[80,128]{1,0:T(8,128)(2,1)S(1)}, bf16[80,128]{1,0:T(8,128)(2,1)}, u32[]{:S(2)}) copy-start(bf16[80,128]{1,0:T(8,128)(2,1)} %part_ref.1) | copy-start | bytes 61444

commit v2 on v1

--- a/solution.py
+++ b/solution.py
@@ -104,9 +104,9 @@
     pl.semaphore_wait(barrier, nd - 1)
 
     copies = []
-    for o in range(1, n):
+
+    def send_in(j, o):
         t = lax.rem(s + o, n)
-        dest = {"shell": t, "batch": b}
         first = pl.multiple_of((t * m + b) * kc, kc)
         pairs = (
             (cls_ref.at[pl.ds(first, kc)], g_cls.at[s]),
@@ -114,13 +114,18 @@
             (tab_ref, g_tab.at[s]),
             (part_ref, g_part.at[b, s]),
         )
-        for j, (src, dst) in enumerate(pairs):
-            copy = pltpu.make_async_remote_copy(
-                src_ref=src, dst_ref=dst, send_sem=in_send.at[j, t], recv_sem=in_recv.at[j, s],
-                device_id=dest, device_id_type=MESH,
-            )
-            copy.start()
-            copies.append(copy)
+        copy = pltpu.make_async_remote_copy(
+            src_ref=pairs[j][0], dst_ref=pairs[j][1], send_sem=in_send.at[j, t], recv_sem=in_recv.at[j, s],
+            device_id={"shell": t, "batch": b}, device_id_type=MESH,
+        )
+        copy.start()
+        copies.append(copy)
+
+    for o in range(1, n):
+        for j in range(3):
+            send_in(j, o)
+    for o in range(1, n):
+        send_in(3, o)
     partner = {"shell": s, "batch": 1 - b}
     pick_copy = pltpu.make_async_remote_copy(
         src_ref=pick_ref, dst_ref=g_pick.at[b], send_sem=pick_sem.at[0], recv_sem=pick_sem.at[1],
@@ -156,10 +161,6 @@
         arrive(0, t)
         arrive(1, t)
         arrive(2, t)
-    for o in range(1, n):
-        t = lax.rem(s + n - o, n)
-        arrive(3, t)
-        relay(g_part.at[b, t], t)
 
     left = lane((rot, 128)) < half
     for t in range(n):
@@ -169,21 +170,27 @@
         inv[t] = jnp.where(left, swap, tab + half).astype(jnp.int32)
         cls32[t] = g_cls[t].astype(F32)
 
-    def rotate(r, carry):
-        at = pl.ds(pl.multiple_of(r * kc, kc), kc)
-        for t in range(n):
-            index = jnp.broadcast_to(fwd[t, pl.ds(r, 1), :], (kc, 128))
-            turned = gather_lanes(cls32[t], index)
-            square = turned * turned
-            high = square.astype(BF16)
-            cols = slice(t * 128, t * 128 + 128)
-            r_s[at, cols] = turned.astype(BF16)
-            hi_s[at, cols] = high
-            lo_s[at, cols] = (square - high.astype(F32)).astype(BF16)
+    def rotate(i, carry):
+        for u in range(2):
+            r = i * 2 + u
+            at = pl.ds(pl.multiple_of(r * kc, kc), kc)
+            for t in range(n):
+                index = jnp.broadcast_to(fwd[t, pl.ds(r, 1), :], (kc, 128))
+                turned = gather_lanes(cls32[t], index)
+                square = turned * turned
+                high = square.astype(BF16)
+                cols = slice(t * 128, t * 128 + 128)
+                r_s[at, cols] = turned.astype(BF16)
+                hi_s[at, cols] = high
+                lo_s[at, cols] = (square - high.astype(F32)).astype(BF16)
         return carry
 
-    lax.fori_loop(0, rot, rotate, 0)
-
+    lax.fori_loop(0, rot // 2, rotate, 0)
+
+    for o in range(1, n):
+        t = lax.rem(s + n - o, n)
+        arrive(3, t)
+        relay(g_part.at[b, t], t)
     pick_copy.wait()
     for o in range(n):
         t = lax.rem(s + o, n)
@@ -262,25 +269,23 @@
     post_s[...] = jnp.exp(sc_s[...] - logev).astype(BF16)
 
     def back(first, index_of):
-        cols = slice(first, first + 256)
+        cols = pl.ds(pl.multiple_of(first, 256), 256)
         frame[...] = jnp.dot(post_s[...], s_s[:, cols], preferred_element_type=F32)
 
-        def step(r, carry):
-            at = pl.ds(pl.multiple_of(r * kc, kc), kc)
-            out = []
-            for q in range(2):
-                index = jnp.broadcast_to(index_of(q, r), (kc, 128))
-                out.append(carry[q] + gather_lanes(frame[at, q * 128 : q * 128 + 128], index))
+        def step(i, carry):
+            out = list(carry)
+            for u in range(8):
+                r = i * 8 + u
+                at = pl.ds(pl.multiple_of(r * kc, kc), kc)
+                for q in range(2):
+                    index = jnp.broadcast_to(index_of(q, r), (kc, 128))
+                    out[q] = out[q] + gather_lanes(frame[at, q * 128 : q * 128 + 128], index)
             return tuple(out)
 
         zero = jnp.zeros((kc, 128), F32)
-        return lax.fori_loop(0, rot, step, (zero, zero))
+        return lax.fori_loop(0, rot // 8, step, (zero, zero))
 
     left1 = lane((1, 128)) < half
-    for j in range(n // 2):
-        done = back(j * 256, lambda q, r: inv[2 * j + q, pl.ds(r, 1), :])
-        for q in range(2):
-            o_mine[2 * j + q, 0:kc, :] = done[q].astype(BF16)
     left_h = lane((kc // 2, 128)) < half
     for j in range(n // 4):
         done = back(
@@ -295,14 +300,33 @@
             o_mine[4 * j + 2 * q, at, :] = jnp.where(left_h, low, pltpu.roll(high, half, 1)).astype(BF16)
             o_mine[4 * j + 2 * q + 1, at, :] = jnp.where(left_h, pltpu.roll(low, half, 1), high).astype(BF16)
 
-    for o in range(1, nd):
-        other, dest = peer(o)
-        copy = pltpu.make_async_remote_copy(
-            src_ref=o_mine.at[dest["shell"]], dst_ref=o_all.at[me], send_sem=o_send.at[other],
-            recv_sem=o_recv.at[me], device_id=dest, device_id_type=MESH,
-        )
+    def send_out(t, c):
+        other = t * m + c
+        return pltpu.make_async_remote_copy(
+            src_ref=o_mine.at[t], dst_ref=o_all.at[me], send_sem=o_send.at[other],
+            recv_sem=o_recv.at[me], device_id={"shell": t, "batch": c}, device_id_type=MESH,
+        )
+
+    pairs_of = n // 2
+    for j in range(pairs_of):
+        base = lax.rem(s // 2 + 1 + j, pairs_of) * 2
+        done = back(base * 128, lambda q, r: inv[base + q, pl.ds(r, 1), :])
+        for q in range(2):
+            o_mine[base + q, 0:kc, :] = done[q].astype(BF16)
+        if j < pairs_of - 1:
+            for q in range(2):
+                for c in range(m):
+                    copy = send_out(base + q, c)
+                    copy.start()
+                    sends.append(copy)
+    near = s // 2 * 2 + 1 - lax.rem(s, 2)
+    for c in range(m):
+        copy = send_out(near, c)
         copy.start()
         sends.append(copy)
+    copy = send_out(s, 1 - b)
+    copy.start()
+    sends.append(copy)
     o_all[me] = o_mine[s]
     for o in range(1, nd):
         other = lax.rem(me + nd - o, nd)
@@ -419,7 +443,7 @@
             and shell_of.shape[0] == 64
             and ctf.shape[0] == 8
             and particles.shape[0] % 16 == 0
-            and rot_table.shape[0] % 8 == 0
+            and rot_table.shape[0] % 16 == 0
             and per * rot_table.shape[0] % 128 == 0
         )
         if fits:

time: 65 us -> 43.6 us (0.67)
  Pallas kernels: 58.3 us -> 36.9 us
    pallas_call x1, Pallas kernels: 58.3 us -> 36.9 us  [fast_body(): pl.pallas_call(functools.partial(kernel, n, m, kc, rot), out_shape=(jax.S...]
where the time goes in v2:
time: 43.6 us; the launch traced here: 43.4 us
  Pallas kernels  36.9 us (85%)
  other arithmetic  3.72 us (9%)
  local copies, waits for them, and re-layouts  2.04 us (5%)
  between operations  0.7 us (2%)
    pallas_call x1, Pallas kernels, fast_body(): pl.pallas_call(functools.partial(kernel, n, m, kc, rot), out_shape=(jax.S...  36.9 us
    unnamed x6, local copies, waits for them, and re-layouts  1.38 us
    reduce_sum x1, other arithmetic, fast_body(): jnp.sum(jnp.where(shell_of[:, None] == levels[None, :], sigma2[None, :],...  0.88 us

profile of v2, /device:TPU:0, one launch (start us, length us, event | category | flops | bytes accessed | tf_op | source)
XLA Modules:
  0.0 43.4 jit_solution(13567930265725803927)
XLA Ops:
  0.6 0.0 copy-start
  0.6 0.0 copy-start.1
  0.7 0.9 %select_reduce_fusion.1 = f32[64]{0:T(128)S(1)} fusion(f32[64]{0:T(128)} %param.10, s32[64]{0:T(128)} %param.11), kind=kLoop, calls=%fused_computation.3 | loop fusion | flops 12224 | bytes 768 | tf_op jit(solution)/shard_map/reduce_sum | solution.py:360
  1.6 0.1 pad.1.clone
  1.6 0.7 %pad_maximum_fusion.1.cw_ref = f32[8,128]{1,0:T(8,128)S(1)} fusion(f32[8,64]{1,0:T(8,128)} %param.9, f32[128]{0:T(128)S(1)} %pad.1.clone), kind=kLoop, calls=%fused_computation.7 | loop fusion | flops 1024 | bytes 6656 | tf_op jit(solution)/shard_map/concatenate | solution.py:362
  2.3 0.7 %and_convert_fusion.pick_ref = bf16[80,128]{1,0:T(8,128)(2,1)S(1)} fusion(s32[128]{0:T(128)S(1)} %and_select_fusion, s32[80]{0:T(128)} %param.13, pred[128]{0:T(512)(128)(4,1)S(1)} %iota_compare_fusion.2), kind=kLoop, calls=%fused_computation.2 | loop fusion | flops 30720 | bytes 21440 | tf_op jit(solution)/shard_map/convert_element_type | solution.py:364
  3.1 0.7 %fusion = (bf16[48,64]{1,0:T(8,128)(2,1)S(1)}, s32[48,64]{1,0:T(8,128)S(1)}) fusion(s32[48,64]{1,0:T(8,128)} %param.12, s32[]{:T(128)S(6)} %mul.6), kind=kLoop, calls=%fused_computation.12 | loop fusion | flops 6144 | bytes 30724 | tf_op jit(solution)/shard_map/convert
  3.8 0.6 %select_reduce_fusion = s32[48,64]{1,0:T(8,128)S(1)} fusion(s32[48,64]{1,0:T(8,128)S(1)} %get-tuple-element.16), kind=kLoop, calls=%fused_computation | loop fusion | flops 586752 | bytes 24576 | tf_op jit(solution)/shard_map/reduce_sum | solution.py:355
  4.4 0.1 pad_maximum_fusion.tab_ref
  4.5 0.0 copy-done
  4.5 0.0 copy-done.1
  4.5 36.9 %shard_map.94 = (f32[256,128]{1,0:T(8,128)S(1)}, f32[256,64]{1,0:T(8,128)S(1)}, f32[1,160]{1,0:T(1,128)S(1)}) custom-call(bf16[80,128]{1,0:T(8,128)(2,1)S(1)} %copy-done.1, bf16[48,128]{1,0:T(8,128)(2,1)S(1)} %pad_maximum_fusion.tab_ref, bf16[256,128]{1,0:T(8,128)(2,1)S(1)} %copy-done, f32[8,128]{1,0:T(8,128)S(1)} %pad_maximum_fusion.1.cw_ref, ...), custom_call_target="tpu_custom_call" | custom-call | tf_op jit(solution)/shard_map/pallas_call | solution.py:371
  41.4 0.6 %dynamic-slice_bitcast_fusion = f32[80]{0:T(128)} fusion(f32[1,160]{1,0:T(1,128)S(1)} %get-tuple-element.8, s32[]{:T(128)S(6)} %select_n.25), kind=kLoop, calls=%fused_computation.9 | loop fusion | bytes 644 | tf_op jit(solution)/shard_map/dynamic_slice | solution.py:416
  42.0 0.7 %copy.11 = f32[256,64]{0,1:T(8,128)} copy(f32[256,64]{1,0:T(8,128)S(1)} %get-tuple-element.13) | data formatting | bytes 131072
  42.7 0.7 %copy.13 = f32[256,128]{1,0:T(8,128)} copy(f32[256,128]{1,0:T(8,128)S(1)} %get-tuple-element.20) | data formatting | bytes 262144
  (4 shorter events, 0.0 us)
Async XLA Ops:
  0.6 3.9 %copy-start = (bf16[256,128]{1,0:T(8,128)(2,1)S(1)}, bf16[256,128]{1,0:T(8,128)(2,1)}, u32[]{:S(2)}) copy-start(bf16[256,128]{1,0:T(8,128)(2,1)} %cls_ref.1) | copy-start | bytes 196612
  0.6 3.9 %copy-start.1 = (bf16[80,128]{1,0:T(8,128)(2,1)S(1)}, bf16[80,128]{1,0:T(8,128)(2,1)}, u32[]{:S(2)}) copy-start(bf16[80,128]{1,0:T(8,128)(2,1)} %part_ref.1) | copy-start | bytes 61444

commit v3 on v2

--- a/solution.py
+++ b/solution.py
@@ -79,9 +79,9 @@
 
 
 def kernel(
-    n, m, kc, rot, part_ref, tab_ref, cls_ref, cw_ref, pick_ref,
+    n, m, kc, rot, part_ref, cls_ref, ctf_ref, sigma_ref, shell_ref, table_ref, group_ref,
     sums_ref, wts_ref, logev_ref,
-    g_part, g_tab, g_cls, g_cw, g_pick, fwd, inv, cls32, w_s, s_s, p_s, r_s, hi_s, lo_s, sc_s, post_s, frame,
+    tab_ref, cw_ref, grp_ref, g_grp, square, w_out, g_part, g_tab, g_cls, g_cw, g_pick, fwd, inv, cls32, w_s, s_s, p_s, r_s, hi_s, lo_s, sc_s, post_s, frame,
     st_mine, st_all, o_mine, o_all,
     in_send, in_recv, relay_send, relay_recv, pick_sem, st_send, st_recv, o_send, o_recv,
 ):
@@ -101,6 +101,32 @@
     barrier = pltpu.get_barrier_semaphore()
     for o in range(1, nd):
         pl.semaphore_signal(barrier, inc=1, device_id=peer(o)[1], device_id_type=MESH)
+
+    def sub(shape):
+        return lax.broadcasted_iota(jnp.int32, shape, 0)
+
+    table = (table_ref[...] - s * half).astype(F32)
+    table = jnp.concatenate([table, jnp.zeros_like(table)], axis=1)
+    tall = jnp.concatenate([table, jnp.zeros((128 - rot, 128), F32)], axis=0)
+    square[...] = tall.T
+    spots = sub((half, 128)).astype(F32)
+    found = jnp.zeros((half, 128), F32)
+    for c in range(half):
+        found = jnp.where(square[c : c + 1, :] == spots, float(c), found)
+    back_table = jnp.concatenate([found, jnp.zeros_like(found)], axis=0).T[:rot]
+    tab_ref[...] = (table + pltpu.roll(back_table, half, 1)).astype(BF16)
+    levels = sigma_ref.shape[1]
+    chosen_level = (shell_ref[...] == sub((levels, half))).astype(F32).astype(BF16)
+    one, two, three = split3(sigma_ref[...])
+    order = sub((8, levels))
+    stack = jnp.where(order == 0, one, jnp.where(order == 1, two, jnp.where(order == 2, three, 0.0)))
+    chosen = jnp.dot(stack.astype(BF16), chosen_level, preferred_element_type=F32)
+    weight = 1.0 / jnp.sum(chosen, axis=0, keepdims=True)
+    ctf = ctf_ref[...]
+    cw_ref[...] = jnp.concatenate([ctf, jnp.broadcast_to(weight, ctf.shape)], axis=1)
+    grp_ref[...] = jnp.zeros_like(grp_ref)
+    grp_ref[:, :rows] = group_ref[...]
+
     pl.semaphore_wait(barrier, nd - 1)
 
     copies = []
@@ -128,7 +154,7 @@
         send_in(3, o)
     partner = {"shell": s, "batch": 1 - b}
     pick_copy = pltpu.make_async_remote_copy(
-        src_ref=pick_ref, dst_ref=g_pick.at[b], send_sem=pick_sem.at[0], recv_sem=pick_sem.at[1],
+        src_ref=grp_ref, dst_ref=g_grp.at[b], send_sem=pick_sem.at[0], recv_sem=pick_sem.at[1],
         device_id=partner, device_id_type=MESH,
     )
     pick_copy.start()
@@ -144,7 +170,7 @@
 
     relay(part_ref, s)
     g_part[b, s] = part_ref[...]
-    g_pick[b] = pick_ref[...]
+    g_grp[b] = grp_ref[...]
     g_tab[s] = tab_ref[...]
     g_cw[s] = cw_ref[...]
     g_cls[s] = cls_ref[pl.ds(pl.multiple_of(me * kc, kc), kc), :]
@@ -177,12 +203,12 @@
             for t in range(n):
                 index = jnp.broadcast_to(fwd[t, pl.ds(r, 1), :], (kc, 128))
                 turned = gather_lanes(cls32[t], index)
-                square = turned * turned
-                high = square.astype(BF16)
+                power = turned * turned
+                high = power.astype(BF16)
                 cols = slice(t * 128, t * 128 + 128)
                 r_s[at, cols] = turned.astype(BF16)
                 hi_s[at, cols] = high
-                lo_s[at, cols] = (square - high.astype(F32)).astype(BF16)
+                lo_s[at, cols] = (power - high.astype(F32)).astype(BF16)
         return carry
 
     lax.fori_loop(0, rot // 2, rotate, 0)
@@ -192,6 +218,10 @@
         arrive(3, t)
         relay(g_part.at[b, t], t)
     pick_copy.wait()
+    place = sub((128, 128))
+    for c in range(m):
+        member = (g_grp[c] == (place & 7)) & (place < 24)
+        g_pick[c] = member.astype(F32).T[:rows].astype(BF16)
     for o in range(n):
         t = lax.rem(s + o, n)
         pltpu.make_async_remote_copy(
@@ -265,7 +295,7 @@
     top = jnp.max(peaks, axis=0, keepdims=True)
     whole = jnp.sum(st_all[:, 1, :] * jnp.exp(peaks - top), axis=0, keepdims=True)
     logev = top + jnp.log(whole)
-    logev_ref[...] = logev
+    logev_ref[...] = jnp.where(b == 0, logev[:, :rows], logev[:, rows:])
     post_s[...] = jnp.exp(sc_s[...] - logev).astype(BF16)
 
     def back(first, index_of):
@@ -337,8 +367,10 @@
     for d in range(nd):
         sums_ref[d * kc : d * kc + kc, :] = o_all[d, 0:kc, :].astype(F32)
         packed = o_all[d, kc : kc + kc // 2, :].astype(F32)
-        wts_ref[d * kc : d * kc + kc // 2, :] = packed[:, :half]
-        wts_ref[d * kc + kc // 2 : d * kc + kc, :] = pltpu.roll(packed, half, 1)[:, :half]
+        w_out[d * kc : d * kc + kc // 2, :] = packed
+        w_out[d * kc + kc // 2 : d * kc + kc, :] = pltpu.roll(packed, half, 1)
+    for d in range(nd * kc // 128):
+        wts_ref[:, d * 128 : d * 128 + 128] = w_out[d * 128 : d * 128 + 128, :].T[:half]
     for copy in copies + relays + sends:
         copy.wait_send()
 
@@ -350,18 +382,6 @@
     k = classes.shape[0]
     groups = ctf.shape[0]
     kc = k // (n * m)
-    table = rot_table - lax.axis_index("shell") * width
-    spots = jnp.arange(width, dtype=jnp.int32)
-    inverse = jnp.sum(
-        jnp.where(table[:, :, None] == spots[None, None, :], spots[None, :, None], 0), axis=1
-    )
-    tabs = jnp.concatenate([table, inverse], axis=1).astype(BF16)
-    levels = jnp.arange(sigma2.shape[0], dtype=jnp.int32)
-    chosen = jnp.sum(jnp.where(shell_of[:, None] == levels[None, :], sigma2[None, :], 0.0), axis=1)
-    weight = 1.0 / chosen
-    cw = jnp.concatenate([ctf, jnp.broadcast_to(weight[None, :], ctf.shape)], axis=1)
-    lanes = jnp.arange(128, dtype=jnp.int32)
-    pick = ((ctf_group[:, None] == (lanes % groups)[None, :]) & (lanes < 3 * groups)[None, :]).astype(BF16)
     total_rows = m * rows
     big = kc * rot
     nd = n * m
@@ -372,12 +392,18 @@
         functools.partial(kernel, n, m, kc, rot),
         out_shape=(
             jax.ShapeDtypeStruct((k, 128), F32),
-            jax.ShapeDtypeStruct((k, width), F32),
-            jax.ShapeDtypeStruct((1, total_rows), F32),
+            jax.ShapeDtypeStruct((width, k), F32),
+            jax.ShapeDtypeStruct((1, rows), F32),
         ),
-        in_specs=[vmem] * 5,
+        in_specs=[vmem] * 7,
         out_specs=(vmem,) * 3,
         scratch_shapes=[
+            pltpu.VMEM((rot, 128), BF16),
+            pltpu.VMEM((groups, 128), F32),
+            pltpu.VMEM((1, 128), jnp.int32),
+            pltpu.VMEM((m, 1, 128), jnp.int32),
+            pltpu.VMEM((128, 128), F32),
+            pltpu.VMEM((k, 128), F32),
             pltpu.VMEM((m, n, rows, 128), BF16),
             pltpu.VMEM((n, rot, 128), BF16),
             pltpu.VMEM((n, kc, 128), BF16),
@@ -412,9 +438,8 @@
         compiler_params=pltpu.CompilerParams(
             collective_id=0, has_side_effects=True, vmem_limit_bytes=48 * 1024 * 1024
         ),
-    )(particles, tabs, classes, cw, pick)
-    mine = lax.dynamic_slice(logev[0], (lax.axis_index("batch") * rows,), (rows,))
-    return sums, wts, mine
+    )(particles, classes, ctf, sigma2[None, :], shell_of[None, :], rot_table, ctf_group[None, :])
+    return sums, wts.T, logev[0]
 
 
 def solution(mesh):
@@ -443,6 +468,10 @@
             and shell_of.shape[0] == 64
             and ctf.shape[0] == 8
             and particles.shape[0] % 16 == 0
+            and particles.shape[0] <= 128
+            and rot_table.shape[0] <= 128
+            and classes.shape[0] % 128 == 0
+            and sigma2.shape[0] % 8 == 0
             and rot_table.shape[0] % 16 == 0
             and per * rot_table.shape[0] % 128 == 0
         )

time: 43.6 us -> 42.6 us (0.977)
  other arithmetic: 3.72 us -> 0 us
  local copies, waits for them, and re-layouts: 2.04 us -> 4.77 us
    unnamed x6 -> x17, local copies, waits for them, and re-layouts: 1.38 us -> 4.77 us
    reduce_sum x2 -> x0, other arithmetic: 1.44 us -> none  [the longest x1 0.88 us: fast_body(): jnp.sum(jnp.where(shell_of[:, None] == levels[None, :], sigma2[None, :],...]
    concatenate x2 -> x0, other arithmetic: 0.78 us -> none  [the longest x1 0.7 us: fast_body(): jnp.concatenate([ctf, jnp.broadcast_to(weight[None, :], ctf.shape)], axis=1)]
    another operation x2 -> x0, other arithmetic: 0.75 us -> none
    convert_element_type x1 -> x0, other arithmetic: 0.73 us -> none  [fast_body(): ((ctf_group[:, None] == (lanes % groups)[None, :]) & (lanes < 3 * groups)...]
    dynamic_slice x1 -> x0, local copies, waits for them, and re-layouts: 0.59 us -> none  [fast_body(): lax.dynamic_slice(logev[0], (lax.axis_index('batch') * rows,), (rows,))]
where the time goes in v3:
time: 42.6 us; the launch traced here: 42.3 us
  Pallas kernels  36.9 us (87%)
  local copies, waits for them, and re-layouts  4.77 us (11%)
  between operations  0.68 us (2%)
    pallas_call x1, Pallas kernels, fast_body(): pl.pallas_call(functools.partial(kernel, n, m, kc, rot), out_shape=(jax.S...  36.9 us
    unnamed x17, local copies, waits for them, and re-layouts  4.77 us

profile of v3, /device:TPU:0, one launch (start us, length us, event | category | flops | bytes accessed | tf_op | source)
XLA Modules:
  0.0 42.3 jit_solution(12069884972160042012)
XLA Ops:
  0.6 0.0 copy-start.3
  0.6 0.0 copy-start.4
  0.7 0.0 copy-start.5
  0.7 0.0 copy-start.6
  0.7 0.6 %copy-done.3 = f32[8,64]{1,0:T(8,128)S(1)} copy-done((f32[8,64]{1,0:T(8,128)S(1)}, f32[8,64]{1,0:T(8,128)}, u32[]{:S(2)}) %copy-start.3) | copy-done | bytes 2072
  1.3 0.0 copy-done.4
  1.3 0.0 copy-done.5
  1.3 0.0 copy-done.6
  1.3 0.0 copy-start
  1.3 0.8 %copy-done = bf16[256,128]{1,0:T(8,128)(2,1)S(1)} copy-done((bf16[256,128]{1,0:T(8,128)(2,1)S(1)}, bf16[256,128]{1,0:T(8,128)(2,1)}, u32[]{:S(2)}) %copy-start) | copy-done | bytes 65560
  2.2 0.0 copy-start.1
  2.2 0.7 %copy-done.1 = s32[48,64]{1,0:T(8,128)S(1)} copy-done((s32[48,64]{1,0:T(8,128)S(1)}, s32[48,64]{1,0:T(8,128)}, u32[]{:S(2)}) %copy-start.1) | copy-done | bytes 12312
  2.9 0.0 copy-start.2
  2.9 0.7 %copy-done.2 = bf16[80,128]{1,0:T(8,128)(2,1)S(1)} copy-done((bf16[80,128]{1,0:T(8,128)(2,1)S(1)}, bf16[80,128]{1,0:T(8,128)(2,1)}, u32[]{:S(2)}) %copy-start.2) | copy-done | bytes 20504
  3.6 36.9 %shard_map.94 = (f32[256,128]{1,0:T(8,128)S(1)}, f32[64,256]{1,0:T(8,128)S(1)}, f32[1,80]{1,0:T(1,128)S(1)}) custom-call(bf16[80,128]{1,0:T(8,128)(2,1)S(1)} %copy-done.2, bf16[256,128]{1,0:T(8,128)(2,1)S(1)} %copy-done, f32[8,64]{1,0:T(8,128)S(1)} %copy-done.3, f32[1,64]{1,0:T(1,128)S(1)} %bitcast.6, s32[1,64]{1,0:T(1,128)S(1)} %bitcast.7, ...), custom_call_target="tpu_custom_call" | custom-call | tf_op jit(solution)/shard_map/pallas_call | solution.py:391
  40.5 0.7 %copy.13 = f32[256,128]{1,0:T(8,128)} copy(f32[256,128]{1,0:T(8,128)S(1)} %get-tuple-element.12) | data formatting | bytes 262144
  41.2 0.6 %copy.14 = f32[256,64]{0,1:T(8,128)} copy(f32[256,64]{0,1:T(8,128)S(1)} %bitcast.5) | data formatting | bytes 131072
  41.8 0.5 %copy.15 = f32[80]{0:T(128)} copy(f32[80]{0:T(128)S(1)} %bitcast.9) | data formatting | bytes 640
Async XLA Ops:
  0.6 0.7 %copy-start.3 = (f32[8,64]{1,0:T(8,128)S(1)}, f32[8,64]{1,0:T(8,128)}, u32[]{:S(2)}) copy-start(f32[8,64]{1,0:T(8,128)} %ctf_ref.1) | copy-start | bytes 6148
  0.6 0.7 %copy-start.4 = (f32[64]{0:T(128)S(1)}, f32[64]{0:T(128)}, u32[]{:S(2)}) copy-start(f32[64]{0:T(128)} %param.10) | copy-start | bytes 772
  0.7 0.7 %copy-start.5 = (s32[64]{0:T(128)S(1)}, s32[64]{0:T(128)}, u32[]{:S(2)}) copy-start(s32[64]{0:T(128)} %param.11) | copy-start | bytes 772
  0.7 0.7 %copy-start.6 = (s32[80]{0:T(128)S(1)}, s32[80]{0:T(128)}, u32[]{:S(2)}) copy-start(s32[80]{0:T(128)} %param.13) | copy-start | bytes 964
  1.3 0.8 %copy-start = (bf16[256,128]{1,0:T(8,128)(2,1)S(1)}, bf16[256,128]{1,0:T(8,128)(2,1)}, u32[]{:S(2)}) copy-start(bf16[256,128]{1,0:T(8,128)(2,1)} %cls_ref.1) | copy-start | bytes 196612
  2.2 0.7 %copy-start.1 = (s32[48,64]{1,0:T(8,128)S(1)}, s32[48,64]{1,0:T(8,128)}, u32[]{:S(2)}) copy-start(s32[48,64]{1,0:T(8,128)} %table_ref.1) | copy-start | bytes 36868
  2.9 0.7 %copy-start.2 = (bf16[80,128]{1,0:T(8,128)(2,1)S(1)}, bf16[80,128]{1,0:T(8,128)(2,1)}, u32[]{:S(2)}) copy-start(bf16[80,128]{1,0:T(8,128)(2,1)} %part_ref.1) | copy-start | bytes 61444

commit v4 on v3

--- a/solution.py
+++ b/solution.py
@@ -79,8 +79,9 @@
 
 
 def kernel(
-    n, m, kc, rot, part_ref, cls_ref, ctf_ref, sigma_ref, shell_ref, table_ref, group_ref,
+    n, m, kc, rot, part_in, cls_in, ctf_in, sigma_in, shell_in, table_in, group_in,
     sums_ref, wts_ref, logev_ref,
+    part_ref, cls_ref, ctf_ref, sigma_ref, shell_ref, table_ref, group_ref, load_sem,
     tab_ref, cw_ref, grp_ref, g_grp, square, w_out, g_part, g_tab, g_cls, g_cw, g_pick, fwd, inv, cls32, w_s, s_s, p_s, r_s, hi_s, lo_s, sc_s, post_s, frame,
     st_mine, st_all, o_mine, o_all,
     in_send, in_recv, relay_send, relay_recv, pick_sem, st_send, st_recv, o_send, o_recv,
@@ -98,6 +99,17 @@
         other = lax.rem(me + o, nd)
         return other, {"shell": other // m, "batch": lax.rem(other, m)}
 
+    loads = [
+        pltpu.make_async_copy(src, dst, load_sem.at[j])
+        for j, (src, dst) in enumerate(
+            (
+                (table_in, table_ref), (sigma_in, sigma_ref), (shell_in, shell_ref), (ctf_in, ctf_ref),
+                (group_in, group_ref), (cls_in, cls_ref), (part_in, part_ref),
+            )
+        )
+    ]
+    for load in loads:
+        load.start()
     barrier = pltpu.get_barrier_semaphore()
     for o in range(1, nd):
         pl.semaphore_signal(barrier, inc=1, device_id=peer(o)[1], device_id_type=MESH)
@@ -105,6 +117,8 @@
     def sub(shape):
         return lax.broadcasted_iota(jnp.int32, shape, 0)
 
+    for load in loads:
+        load.wait()
     table = (table_ref[...] - s * half).astype(F32)
     table = jnp.concatenate([table, jnp.zeros_like(table)], axis=1)
     tall = jnp.concatenate([table, jnp.zeros((128 - rot, 128), F32)], axis=0)
@@ -197,8 +211,8 @@
         cls32[t] = g_cls[t].astype(F32)
 
     def rotate(i, carry):
-        for u in range(2):
-            r = i * 2 + u
+        for u in range(4):
+            r = i * 4 + u
             at = pl.ds(pl.multiple_of(r * kc, kc), kc)
             for t in range(n):
                 index = jnp.broadcast_to(fwd[t, pl.ds(r, 1), :], (kc, 128))
@@ -211,7 +225,7 @@
                 lo_s[at, cols] = (power - high.astype(F32)).astype(BF16)
         return carry
 
-    lax.fori_loop(0, rot // 2, rotate, 0)
+    lax.fori_loop(0, rot // 4, rotate, 0)
 
     for o in range(1, n):
         t = lax.rem(s + n - o, n)
@@ -254,7 +268,7 @@
         before = ctf_part
 
     nt = (((1,), (1,)), ((), ()))
-    chunk = 128
+    chunk = 384
     big = kc * rot
 
     def score(i, peak):
@@ -304,8 +318,8 @@
 
         def step(i, carry):
             out = list(carry)
-            for u in range(8):
-                r = i * 8 + u
+            for u in range(24):
+                r = i * 24 + u
                 at = pl.ds(pl.multiple_of(r * kc, kc), kc)
                 for q in range(2):
                     index = jnp.broadcast_to(index_of(q, r), (kc, 128))
@@ -313,7 +327,7 @@
             return tuple(out)
 
         zero = jnp.zeros((kc, 128), F32)
-        return lax.fori_loop(0, rot // 8, step, (zero, zero))
+        return lax.fori_loop(0, rot // 24, step, (zero, zero))
 
     left1 = lane((1, 128)) < half
     left_h = lane((kc // 2, 128)) < half
@@ -365,12 +379,12 @@
             recv_sem=o_recv.at[other], device_id=partner, device_id_type=MESH,
         ).wait_recv()
     for d in range(nd):
-        sums_ref[d * kc : d * kc + kc, :] = o_all[d, 0:kc, :].astype(F32)
+        sums_ref[d * kc : d * kc + kc, :] = o_all[d, 0:kc, :]
         packed = o_all[d, kc : kc + kc // 2, :].astype(F32)
         w_out[d * kc : d * kc + kc // 2, :] = packed
         w_out[d * kc + kc // 2 : d * kc + kc, :] = pltpu.roll(packed, half, 1)
     for d in range(nd * kc // 128):
-        wts_ref[:, d * 128 : d * 128 + 128] = w_out[d * 128 : d * 128 + 128, :].T[:half]
+        wts_ref[:, d * 128 : d * 128 + 128] = w_out[d * 128 : d * 128 + 128, :].T[:half].astype(BF16)
     for copy in copies + relays + sends:
         copy.wait_send()
 
@@ -391,13 +405,21 @@
     sums, wts, logev = pl.pallas_call(
         functools.partial(kernel, n, m, kc, rot),
         out_shape=(
-            jax.ShapeDtypeStruct((k, 128), F32),
-            jax.ShapeDtypeStruct((width, k), F32),
+            jax.ShapeDtypeStruct((k, 128), BF16),
+            jax.ShapeDtypeStruct((width, k), BF16),
             jax.ShapeDtypeStruct((1, rows), F32),
         ),
-        in_specs=[vmem] * 7,
+        in_specs=[pl.BlockSpec(memory_space=pltpu.HBM)] * 7,
         out_specs=(vmem,) * 3,
         scratch_shapes=[
+            pltpu.VMEM((rows, 128), BF16),
+            pltpu.VMEM((k, 128), BF16),
+            pltpu.VMEM((groups, width), F32),
+            pltpu.VMEM((1, sigma2.shape[0]), F32),
+            pltpu.VMEM((1, width), jnp.int32),
+            pltpu.VMEM((rot, width), jnp.int32),
+            pltpu.VMEM((1, rows), jnp.int32),
+            dma((7,)),
             pltpu.VMEM((rot, 128), BF16),
             pltpu.VMEM((groups, 128), F32),
             pltpu.VMEM((1, 128), jnp.int32),
@@ -436,10 +458,10 @@
             dma((nd,)),
         ],
         compiler_params=pltpu.CompilerParams(
-            collective_id=0, has_side_effects=True, vmem_limit_bytes=48 * 1024 * 1024
+            collective_id=0, has_side_effects=True, vmem_limit_bytes=60 * 1024 * 1024
         ),
     )(particles, classes, ctf, sigma2[None, :], shell_of[None, :], rot_table, ctf_group[None, :])
-    return sums, wts.T, logev[0]
+    return sums.astype(F32), wts.T.astype(F32), logev[0]
 
 
 def solution(mesh):
@@ -472,8 +494,8 @@
             and rot_table.shape[0] <= 128
             and classes.shape[0] % 128 == 0
             and sigma2.shape[0] % 8 == 0
-            and rot_table.shape[0] % 16 == 0
-            and per * rot_table.shape[0] % 128 == 0
+            and rot_table.shape[0] % 48 == 0
+            and per * rot_table.shape[0] % 384 == 0
         )
         if fits:
             return fast_body(n, m, *args)

time: 42.6 us -> 37.9 us (0.89)
  local copies, waits for them, and re-layouts: 4.77 us -> 0.54 us
  Pallas kernels: 36.9 us -> 34.3 us
  other arithmetic: 0 us -> 2.14 us
    unnamed x17 -> x5, local copies, waits for them, and re-layouts: 4.77 us -> 0.54 us
    pallas_call x1, Pallas kernels: 36.9 us -> 34.3 us  [fast_body(): pl.pallas_call(functools.partial(kernel, n, m, kc, rot), out_shape=(jax.S...]
    convert_element_type x0 -> x2, other arithmetic: none -> 2.14 us  [fast_body(): return (sums.astype(F32), wts.T.astype(F32), logev[0])]
where the time goes in v4:
time: 37.9 us; the launch traced here: 37.6 us
  Pallas kernels  34.3 us (91%)
  other arithmetic  2.14 us (6%)
  between operations  0.65 us (2%)
  local copies, waits for them, and re-layouts  0.54 us (1%)
    pallas_call x1, Pallas kernels, fast_body(): pl.pallas_call(functools.partial(kernel, n, m, kc, rot), out_shape=(jax.S...  34.3 us
    convert_element_type x2, other arithmetic, fast_body(): return (sums.astype(F32), wts.T.astype(F32), logev[0])  2.14 us

profile of v4, /device:TPU:0, one launch (start us, length us, event | category | flops | bytes accessed | tf_op | source)
XLA Modules:
  0.0 37.6 jit_solution(1087330108959704369)
XLA Ops:
  0.6 34.3 %shard_map.94 = (bf16[256,128]{1,0:T(8,128)(2,1)}, bf16[64,256]{1,0:T(8,128)(2,1)}, f32[1,80]{1,0:T(1,128)}) custom-call(bf16[80,128]{1,0:T(8,128)(2,1)} %part_in.1, bf16[256,128]{1,0:T(8,128)(2,1)} %cls_in.1, f32[8,64]{1,0:T(8,128)} %ctf_in.1, f32[1,64]{1,0:T(1,128)} %bitcast.6, s32[1,64]{1,0:T(1,128)} %bitcast.7, s32[48,64]{1,0:T(8,128)} %table_in.1, ...), custom_call_target="tpu_custom_call" | custom-call | tf_op jit(solution)/shard_map/pallas_call | solution.py:405
  34.9 0.0 copy-start
  34.9 1.5 %convert_element_type.9 = f32[256,128]{1,0:T(8,128)} convert(bf16[256,128]{1,0:T(8,128)(2,1)} %get-tuple-element.6) | non-fusion elementwise | flops 32768 | bytes 196608 | tf_op jit(solution)/shard_map/convert_element_type | solution.py:464
  36.5 0.0 copy-done
  36.5 0.0 copy-start.1
  36.5 0.6 %convert_bitcast_fusion = f32[256,64]{0,1:T(8,128)} fusion(bf16[64,256]{1,0:T(8,128)(2,1)S(1)} %copy-done), kind=kLoop, calls=%fused_computation | loop fusion | flops 16384 | bytes 98304 | tf_op jit(solution)/shard_map/convert_element_type | solution.py:464
  37.1 0.0 copy-done.1
  37.1 0.5 %copy.11 = f32[80]{0:T(128)} copy(f32[80]{0:T(128)S(1)} %bitcast.9) | data formatting | bytes 640
Async XLA Ops:
  34.9 1.5 %copy-start = (bf16[64,256]{1,0:T(8,128)(2,1)S(1)}, bf16[64,256]{1,0:T(8,128)(2,1)}, u32[]{:S(2)}) copy-start(bf16[64,256]{1,0:T(8,128)(2,1)} %get-tuple-element.7) | copy-start | bytes 98308
  36.5 0.7 %copy-start.1 = (f32[1,80]{1,0:T(1,128)S(1)}, f32[1,80]{1,0:T(1,128)}, u32[]{:S(2)}) copy-start(f32[1,80]{1,0:T(1,128)} %get-tuple-element.8) | copy-start | bytes 964

commit v5 on v4

--- a/solution.py
+++ b/solution.py
@@ -272,7 +272,7 @@
     big = kc * rot
 
     def score(i, peak):
-        at = pl.ds(pl.multiple_of(i * chunk, chunk), chunk)
+        at = pl.ds(i * chunk, chunk)
         cross = lax.dot_general(r_s[at, :], w_s[...], nt, preferred_element_type=F32)
         pen = lax.dot_general(hi_s[at, :], p_s[...], nt, preferred_element_type=F32)
         pen = pen + lax.dot_general(lo_s[at, :], p_s[...], nt, preferred_element_type=F32)
@@ -283,7 +283,9 @@
         sc_s[at, :] = total
         return jnp.maximum(peak, jnp.max(total, axis=0, keepdims=True))
 
-    peak = lax.fori_loop(0, big // chunk, score, jnp.full((1, total_rows), -jnp.inf, F32))
+    peak = jnp.full((1, total_rows), -jnp.inf, F32)
+    for i in range(big // chunk):
+        peak = score(i, peak)
     summed = jnp.sum(jnp.exp(sc_s[...] - peak), axis=0, keepdims=True)
     st_mine[0:1, :] = peak
     st_mine[1:2, :] = summed
@@ -318,16 +320,15 @@
 
         def step(i, carry):
             out = list(carry)
-            for u in range(24):
-                r = i * 24 + u
-                at = pl.ds(pl.multiple_of(r * kc, kc), kc)
+            for r in range(rot):
+                at = pl.ds(r * kc, kc)
                 for q in range(2):
                     index = jnp.broadcast_to(index_of(q, r), (kc, 128))
                     out[q] = out[q] + gather_lanes(frame[at, q * 128 : q * 128 + 128], index)
             return tuple(out)
 
         zero = jnp.zeros((kc, 128), F32)
-        return lax.fori_loop(0, rot // 24, step, (zero, zero))
+        return step(0, (zero, zero))
 
     left1 = lane((1, 128)) < half
     left_h = lane((kc // 2, 128)) < half

time: 37.9 us -> 36.1 us (0.953)
  Pallas kernels: 34.3 us -> 32.6 us
    pallas_call x1, Pallas kernels: 34.3 us -> 32.6 us  [fast_body(): pl.pallas_call(functools.partial(kernel, n, m, kc, rot), out_shape=(jax.S...]
where the time goes in v5:
time: 36.1 us; the launch traced here: 35.9 us
  Pallas kernels  32.6 us (90%)
  other arithmetic  2.14 us (6%)
  between operations  0.65 us (2%)
  local copies, waits for them, and re-layouts  0.54 us (1%)
    pallas_call x1, Pallas kernels, fast_body(): pl.pallas_call(functools.partial(kernel, n, m, kc, rot), out_shape=(jax.S...  32.6 us
    convert_element_type x2, other arithmetic, fast_body(): return (sums.astype(F32), wts.T.astype(F32), logev[0])  2.14 us

profile of v5, /device:TPU:0, one launch (start us, length us, event | category | flops | bytes accessed | tf_op | source)
XLA Modules:
  0.0 35.9 jit_solution(8488977660830830279)
XLA Ops:
  0.6 32.6 %shard_map.94 = (bf16[256,128]{1,0:T(8,128)(2,1)}, bf16[64,256]{1,0:T(8,128)(2,1)}, f32[1,80]{1,0:T(1,128)}) custom-call(bf16[80,128]{1,0:T(8,128)(2,1)} %part_in.1, bf16[256,128]{1,0:T(8,128)(2,1)} %cls_in.1, f32[8,64]{1,0:T(8,128)} %ctf_in.1, f32[1,64]{1,0:T(1,128)} %bitcast.6, s32[1,64]{1,0:T(1,128)} %bitcast.7, s32[48,64]{1,0:T(8,128)} %table_in.1, ...), custom_call_target="tpu_custom_call" | custom-call | tf_op jit(solution)/shard_map/pallas_call | solution.py:406
  33.2 0.0 copy-start
  33.2 1.5 %convert_element_type.9 = f32[256,128]{1,0:T(8,128)} convert(bf16[256,128]{1,0:T(8,128)(2,1)} %get-tuple-element.6) | non-fusion elementwise | flops 32768 | bytes 196608 | tf_op jit(solution)/shard_map/convert_element_type | solution.py:465
  34.7 0.0 copy-done
  34.7 0.0 copy-start.1
  34.7 0.6 %convert_bitcast_fusion = f32[256,64]{0,1:T(8,128)} fusion(bf16[64,256]{1,0:T(8,128)(2,1)S(1)} %copy-done), kind=kLoop, calls=%fused_computation | loop fusion | flops 16384 | bytes 98304 | tf_op jit(solution)/shard_map/convert_element_type | solution.py:465
  35.4 0.0 copy-done.1
  35.4 0.5 %copy.11 = f32[80]{0:T(128)} copy(f32[80]{0:T(128)S(1)} %bitcast.9) | data formatting | bytes 640
Async XLA Ops:
  33.2 1.5 %copy-start = (bf16[64,256]{1,0:T(8,128)(2,1)S(1)}, bf16[64,256]{1,0:T(8,128)(2,1)}, u32[]{:S(2)}) copy-start(bf16[64,256]{1,0:T(8,128)(2,1)} %get-tuple-element.7) | copy-start | bytes 98308
  34.7 0.7 %copy-start.1 = (f32[1,80]{1,0:T(1,128)S(1)}, f32[1,80]{1,0:T(1,128)}, u32[]{:S(2)}) copy-start(f32[1,80]{1,0:T(1,128)} %get-tuple-element.8) | copy-start | bytes 964
